TPU v7x, 32 devices: a whole 2x2x4 slice. The times are simulated.
32 devices in a mesh: owner: 4 (over x, core), rows: 8 (over z, y).
Axes of the slice: x: 2, y: 2, z: 4, core: 2. Of those that a mesh axis runs over, the one named last changes fastest.
Arguments:
- train_gate: float32 [128, 2048, 768], P('owner', 'rows'), may hold values from -0.1875 to 0.1875
- train_up: float32 [128, 2048, 768], P('owner', 'rows'), may hold values from -0.1875 to 0.1875
- router_weight: float32 [2048, 128], P('rows', 'owner'), may hold values from -0.125 to 0.125
- router_gain: float32 [2048], P('rows'), may hold values from 0.25 to 1.75
Outputs:
- ready_gate: bfloat16 [128, 2048, 768], P(('owner', 'rows'))
- ready_up: bfloat16 [128, 2048, 768], P(('owner', 'rows'))
- scale_gate: float32 [128, 768], P(('owner', 'rows'))
- scale_up: float32 [128, 768], P(('owner', 'rows'))
- serve_router: bfloat16 [2048, 128], replicated
All inputs are finite; a program needn't handle non-finite values.
Results may differ from a plain program's by a relative error of at most 0.001.
Values may be sent and summed in bfloat16 or wider, within the bound.
No kernel may reach another device: no remote copies, remote signals or barrier semaphores. Data moves between devices by JAX's collectives and lax.ppermute only.
A program may use at most 192 MiB of HBM per device.

v0:
```python
import jax
import jax.numpy as jnp
from jax import lax
from jax.sharding import PartitionSpec as P


def on_device(train_gate, train_up, router_weight, router_gain):
    total_gate, total_up = lax.psum(
        (jnp.sum(train_gate * train_gate, axis=1), jnp.sum(train_up * train_up, axis=1)), "rows"
    )
    scale_gate = jnp.sqrt(total_gate)
    scale_up = jnp.sqrt(total_up)
    narrow_gate, narrow_up = (
        (train_gate / jnp.expand_dims(scale_gate, 1)).astype(jnp.bfloat16),
        (train_up / jnp.expand_dims(scale_up, 1)).astype(jnp.bfloat16),
    )
    ready_gate, ready_up = (
        lax.all_to_all(narrow_gate, "rows", split_axis=0, concat_axis=1, tiled=True),
        lax.all_to_all(narrow_up, "rows", split_axis=0, concat_axis=1, tiled=True),
    )
    scale_gate = lax.dynamic_slice_in_dim(
        scale_gate, lax.axis_index("rows") * ready_gate.shape[0], ready_gate.shape[0], axis=0
    )
    scale_up = lax.dynamic_slice_in_dim(
        scale_up, lax.axis_index("rows") * ready_up.shape[0], ready_up.shape[0], axis=0
    )
    part_router = (router_weight * router_gain[:, None]).astype(jnp.bfloat16)
    row_router = lax.all_gather(part_router, "rows", axis=0, tiled=True)
    serve_router = lax.all_gather(row_router, "owner", axis=1, tiled=True)
    return (ready_gate, ready_up, scale_gate, scale_up, serve_router)


def solution(mesh):
    return jax.shard_map(
        on_device,
        mesh=mesh,
        in_specs=(
            P("owner", "rows", None),
            P("owner", "rows", None),
            P("rows", "owner"),
            P("rows"),
        ),
        out_specs=(
            P(("owner", "rows"), None, None),
            P(("owner", "rows"), None, None),
            P(("owner", "rows"), None),
            P(("owner", "rows"), None),
            P(),
        ),
        check_vma=False,
    )
```

profile of v0, /device:TPU:0, one launch (start us, length us, event | category | flops | bytes accessed | tf_op | source)
XLA Modules:
  0.0 723.9 jit_solution(15116092223100259474)
XLA Ops:
  7.2 0.0 all-reduce.3.cloned.1.call-start
  7.2 17.3 %multiply_reduce_fusion = (f32[32,768]{1,0:T(8,128)}, f32[32,768]{1,0:T(8,128)}) fusion(f32[32,256,768]{2,1,0:T(8,128)} %param.5, f32[32,256,768]{2,1,0:T(8,128)} %param.4), kind=kLoop, calls=%fused_computation.1 | loop fusion | flops 25116672 | bytes 50528256 | tf_op jit(solution)/shard_map/reduce_sum | solution.py:9
  24.5 0.0 all-reduce.3.cloned.1.call-update
  24.5 73.8 %all-reduce.3.cloned.1.call-done = (f32[32,768]{1,0:T(8,128)}, f32[32,768]{1,0:T(8,128)}) async-done(((f32[32,768]{1,0:T(8,128)}, f32[32,768]{1,0:T(8,128)}), (f32[32,768]{1,0:T(8,128)}, f32[32,768]{1,0:T(8,128)})) %all-reduce.3.cloned.1.call-update) | async-done | bytes 196624 | tf_op jit(solution)/shard_map/psum | solution.py:8
  98.2 0.9 sqrt.6
  99.2 0.0 copy-start
  99.2 13.7 %divide_convert_fusion.1 = bf16[32,256,768]{2,1,0:T(8,128)(2,1)} fusion(f32[32,256,768]{2,1,0:T(8,128)} %param.4, f32[32,768]{1,0:T(8,128)S(1)} %sqrt.6), kind=kLoop, calls=%fused_computation.2 | loop fusion | flops 12582912 | bytes 37847040 | tf_op jit(solution)/shard_map/convert_element_type | solution.py:14
  112.9 5.4 all-to-all-start
  118.2 0.0 copy-done
  118.3 0.0 copy-start.1
  118.3 0.0 copy-start.2
  118.3 13.8 %divide_convert_fusion = bf16[32,256,768]{2,1,0:T(8,128)(2,1)} fusion(f32[32,256,768]{2,1,0:T(8,128)} %param.5, f32[32,768]{1,0:T(8,128)S(1)} %sqrt.7), kind=kLoop, calls=%fused_computation | loop fusion | flops 12582912 | bytes 37847040 | tf_op jit(solution)/shard_map/convert_element_type | solution.py:15
  132.1 257.3 %all-to-all-done = bf16[32,256,768]{2,1,0:T(8,128)(2,1)} async-done(((bf16[32,256,768]{2,1,0:T(8,128)(2,1)}), bf16[32,256,768]{2,1,0:T(8,128)(2,1)}, u32[]{:S(2)}, u32[]{:S(2)}) %all-to-all-start) | async-done | bytes 12582944 | tf_op jit(solution)/shard_map/all_to_all | solution.py:18
  389.4 5.4 all-to-all-start.1
  394.8 0.0 copy-done.1
  394.8 0.0 copy-done.2
  394.8 291.6 %all_gather.6 = bf16[2048,32]{0,1:T(8,128)(2,1)S(1)} all-gather(bf16[256,32]{0,1:T(8,128)(2,1)S(1)} %multiply_convert_fusion), channel_id=1, replica_groups=mesh['owner'=4,'rows'=8] {'rows'}, dimensions={0}, use_global_device_ids=true | all-gather | bytes 147456 | tf_op jit(solution)/shard_map/all_gather | solution.py:28
  686.4 7.1 all_gather.7
  693.5 1.0 copy.14
  694.5 0.6 constant_dynamic-slice_fusion
  695.1 0.6 constant_dynamic-slice_fusion.1
  695.7 10.7 %copy.12 = bf16[8,4,256,768]{3,2,0,1:T(8,128)(2,1)} copy(bf16[8,4,256,768]{3,2,1,0:T(8,128)(2,1)} %bitcast) | data formatting | bytes 25165824 | tf_op jit(solution)/shard_map/all_to_all | solution.py:18
  706.4 0.0 all-to-all-done.1
  706.4 10.7 %copy.13 = bf16[8,4,256,768]{3,2,0,1:T(8,128)(2,1)} copy(bf16[8,4,256,768]{3,2,1,0:T(8,128)(2,1)} %bitcast.3) | data formatting | bytes 25165824 | tf_op jit(solution)/shard_map/all_to_all | solution.py:19
  (2 shorter events, 0.0 us)
Async XLA Ops:
  7.2 91.1 %all-reduce.3.cloned.1.call-start = ((), (), s32[]{:S(2)}) async-start(), calls=%async_computation.2 | async-start | bytes 393216 | tf_op jit(solution)/shard_map/psum | solution.py:8
  99.2 19.1 %copy-start = (f32[32,768]{1,0:T(8,128)S(1)}, f32[32,768]{1,0:T(8,128)}, u32[]{:S(2)}) copy-start(f32[32,768]{1,0:T(8,128)} %get-tuple-element.11) | copy-start | bytes 294916
  112.9 276.5 %all-to-all-start = ((bf16[32,256,768]{2,1,0:T(8,128)(2,1)}), bf16[32,256,768]{2,1,0:T(8,128)(2,1)}, u32[]{:S(2)}, u32[]{:S(2)}) async-start(bf16[32,256,768]{2,1,0:T(8,128)(2,1)} %divide_convert_fusion.1), calls=%async_computation | async-start | bytes 25165824 | tf_op jit(solution)/shard_map/all_to_all | solution.py:18
  118.3 276.5 %copy-start.1 = (f32[256,32]{0,1:T(8,128)S(1)}, f32[256,32]{0,1:T(8,128)}, u32[]{:S(2)}) copy-start(f32[256,32]{0,1:T(8,128)} %param.6) | copy-start | bytes 98308
  118.3 276.5 %copy-start.2 = (f32[256]{0:T(256)S(1)}, f32[256]{0:T(256)}, u32[]{:S(2)}) copy-start(f32[256]{0:T(256)} %param.7) | copy-start | bytes 3076
  389.4 317.0 %all-to-all-start.1 = ((bf16[32,256,768]{2,1,0:T(8,128)(2,1)}), bf16[32,256,768]{2,1,0:T(8,128)(2,1)}, u32[]{:S(2)}, u32[]{:S(2)}) async-start(bf16[32,256,768]{2,1,0:T(8,128)(2,1)} %divide_convert_fusion), calls=%async_computation.1 | async-start | bytes 25165824 | tf_op jit(solution)/shard_map/all_to_all | solution.py:19
Sparse Core Ops, SparseCore 0:
  24.6 73.5 all-reduce.2
where the time goes:
time: 724 us
  waiting for transfers between devices  331 us (46%)
  blocking collectives  299 us (41%)
  other arithmetic  44.7 us (6%)
  local copies, waits for them, and re-layouts  24.5 us (3%)
  between operations  14.1 us (2%)
  starting transfers between devices  10.8 us (1%)
    all_gather x1, blocking collectives, on_device(): row_router = lax.all_gather(part_router, 'rows', axis=0, tiled=True)  292 us
    all_to_all x1, waiting for transfers between devices, on_device(): lax.all_to_all(narrow_gate, 'rows', split_axis=0, concat_axis=1, tiled=True)  257 us
    psum x1, waiting for transfers between devices, on_device(): lax.psum((jnp.sum(train_gate * train_gate, axis=1), jnp.sum(train_up * tr...  73.8 us
    reduce_sum x1, other arithmetic, on_device(): jnp.sum(train_up * train_up, axis=1)  17.3 us
  transfers between devices with their start and end apart: 3, of which 2 were waited for; matrix products, arithmetic and copies ran while one was open for 4% of the time, Pallas kernels for 0%

commit v1 on v0

v1 whole, which is shorter than its diff:
```python
import jax
import jax.numpy as jnp
from jax import lax
from jax.experimental import pallas as pl
from jax.experimental.pallas import tpu as pltpu
from jax.sharding import PartitionSpec as P


def tied(value, *others):
    return lax.optimization_barrier((value, *others))[0]


def shift(value, k):
    n = lax.axis_size("rows")
    return lax.ppermute(value, "rows", [(r, r ^ k) for r in range(n)])


def squares(x):
    return jnp.sum(x * x, axis=2)


def at(x, index):
    return lax.dynamic_index_in_dim(x, index, axis=0, keepdims=False)


def scaled(x, scale):
    return (x / scale[:, None, :]).astype(jnp.bfloat16)


def own_kernel(me_ref, x_ref, scale_ref, out_ref):
    del me_ref
    out_ref[...] = (x_ref[0] / scale_ref[...]).astype(jnp.bfloat16)


def own_piece(x, scale, me):
    n, per, rows, cols = x.shape
    return pl.pallas_call(
        own_kernel,
        grid_spec=pltpu.PrefetchScalarGridSpec(
            num_scalar_prefetch=1,
            grid=(per,),
            in_specs=[
                pl.BlockSpec((1, 1, rows, cols), lambda j, me: (me[0], j, 0, 0)),
                pl.BlockSpec((1, 1, cols), lambda j, me: (j, 0, 0)),
            ],
            out_specs=pl.BlockSpec((1, rows, cols), lambda j, me: (j, me[0], 0)),
        ),
        out_shape=jax.ShapeDtypeStruct((per, n * rows, cols), jnp.bfloat16),
        name="own",
    )(me[None], x, scale[:, None, :])


def place_kernel(source_ref, piece_ref, result_ref, out_ref):
    del source_ref, result_ref
    out_ref[...] = piece_ref[...]


def placed(result, piece, first, source):
    count, rows, cols = piece.shape
    return pl.pallas_call(
        place_kernel,
        grid_spec=pltpu.PrefetchScalarGridSpec(
            num_scalar_prefetch=1,
            grid=(count,),
            in_specs=[
                pl.BlockSpec((1, rows, cols), lambda j, s: (j, 0, 0)),
                pl.BlockSpec(memory_space=pl.ANY),
            ],
            out_specs=pl.BlockSpec(
                (1, rows, cols), lambda j, s: (first + j, s[0], 0)
            ),
        ),
        out_shape=jax.ShapeDtypeStruct(result.shape, result.dtype),
        input_output_aliases={2: 0},
        name="place",
    )(source[None], piece, result)


def gathered_router(weight, gain):
    n = lax.axis_size("rows")
    me = lax.axis_index("rows")
    held = (weight * gain[:, None]).astype(jnp.bfloat16)
    bit, depth = n // 2, 0
    while bit:
        other = shift(held, bit)
        low = (me & bit) == 0
        held = jnp.stack(
            [jnp.where(low, held, other), jnp.where(low, other, held)], axis=depth
        )
        bit, depth = bit // 2, depth + 1
    return held.reshape((-1, weight.shape[1]))


def groups(n):
    near = list(range(1, n // 2))
    far = list(range(n // 2, n))
    half, part = n // 4, n // 8
    return near, far, far[:half], far[half : half + part], far[half + part :]


def on_device(train_gate, train_up, router_weight, router_gain):
    n = lax.axis_size("rows")
    me = lax.axis_index("rows")
    experts, rows, cols = train_gate.shape
    per = experts // n
    gate = train_gate.reshape((n, per, rows, cols))
    up = train_up.reshape((n, per, rows, cols))
    near, far, far_a, far_b, far_c = groups(n)

    first = squares(gate[:, :1]).reshape((n, cols))
    parts = lax.all_to_all(
        jnp.broadcast_to(first[None], (n, n, cols)),
        "rows",
        split_axis=0,
        concat_axis=0,
        tiled=True,
    )
    first_scale = jnp.sqrt(jnp.sum(parts.reshape((n, n, cols)), axis=0))

    got_first = {}

    def send_first(ks, scales):
        last = None
        for k in ks:
            index = me ^ k if last is None else tied(me ^ k, last)
            last = scaled(at(gate, index)[:1], at(scales, index)[None])
            got_first[k] = shift(last, k)
        return last

    last = send_first(far_a, first_scale)
    last = send_first(near, tied(first_scale, last))

    gate_later, up_later, weight = tied((gate, up, router_weight), last)
    router = gathered_router(weight, router_gain)
    sums_gate = squares(gate_later[:, 1:])
    sums_up = squares(up_later)
    sums = jnp.concatenate([sums_gate, sums_up], axis=1)
    last = send_first(far_b + far_c, tied(first_scale, last))
    mine = [at(sums, me)] + [shift(at(sums, me ^ k), k) for k in far + near]
    scale = jnp.sqrt(sum(mine[1:], mine[0]))

    theirs = {k: shift(scale, k) for k in far + near}
    got_gate, got_up = {}, {}
    for k in far + near:
        if per > 1:
            last = scaled(at(gate, me ^ k)[1:], tied(theirs[k], last)[: per - 1])
            got_gate[k] = shift(last, k)
    for k in near + far:
        last = scaled(at(up, me ^ k), tied(theirs[k], last)[per - 1 :])
        got_up[k] = shift(last, k)

    scale, first_scale = tied((scale, first_scale), last)
    scale_gate = jnp.concatenate([at(first_scale, me)[None], scale[: per - 1]])
    scale_up = scale[per - 1 :]

    ready_gate = own_piece(gate, scale_gate, me)
    for k in far_a + near + far_b + far_c:
        ready_gate = placed(ready_gate, got_first[k], 0, me ^ k)
    ready_up = own_piece(up, scale_up, me)
    router = tied(router, ready_gate)
    serve_router = lax.all_gather(router, "owner", axis=1, tiled=True)
    if per > 1:
        for k in far + near:
            ready_gate = placed(ready_gate, got_gate[k], 1, me ^ k)
    for k in near + far:
        ready_up = placed(ready_up, got_up[k], 0, me ^ k)
    return (ready_gate, ready_up, scale_gate, scale_up, serve_router)


def solution(mesh):
    return jax.shard_map(
        on_device,
        mesh=mesh,
        in_specs=(
            P("owner", "rows", None),
            P("owner", "rows", None),
            P("rows", "owner"),
            P("rows"),
        ),
        out_specs=(
            P(("owner", "rows"), None, None),
            P(("owner", "rows"), None, None),
            P(("owner", "rows"), None),
            P(("owner", "rows"), None),
            P(),
        ),
        check_vma=False,
    )
```

time: 724 us -> 724 us (level)
  the two profiles are of different devices: /device:TPU:0 before, /device:TPU:12 now
where the time goes in v1:
time: 724 us; the launch traced here: 722 us
  waiting for transfers between devices  502 us (69%)
  starting transfers between devices  74.1 us (10%)
  Pallas kernels  66.9 us (9%)
  other arithmetic  65.7 us (9%)
    ppermute x38, waiting for transfers between devices, shift(): return lax.ppermute(value, 'rows', [(r, r ^ k) for r in range(n)])  496 us
    ppermute x38, starting transfers between devices, shift(): return lax.ppermute(value, 'rows', [(r, r ^ k) for r in range(n)])  67.9 us
    pallas_call x21, Pallas kernels, placed(): pl.pallas_call(place_kernel, grid_spec=pltpu.PrefetchScalarGridSpec(num_s...  59.1 us
    convert_element_type x21, other arithmetic, scaled(): return (x / scale[:, None, :]).astype(jnp.bfloat16)  44 us
    reduce_sum x3, other arithmetic, squares(): return jnp.sum(x * x, axis=2)  20.9 us
  transfers between devices with their start and end apart: 39, of which 20 were waited for; matrix products, arithmetic and copies ran while one was open for 5% of the time, Pallas kernels for 9%

profile of v1, /device:TPU:12, one launch (start us, length us, event | category | flops | bytes accessed | tf_op | source)
XLA Modules:
  0.0 721.6 jit_solution(12720896495433224765)
XLA Ops:
  4.7 6.2 all-to-all-start
  10.9 5.9 all-to-all-done
  26.9 9.3 %multiply_reduce_fusion = f32[8,4,768]{2,1,0:T(4,128)S(1)} fusion(f32[8,4,256,768]{3,2,1,0:T(8,128)} %bitcast.170), kind=kLoop, calls=%fused_computation | loop fusion | flops 12558336 | bytes 25264128 | tf_op jit(solution)/shard_map/reduce_sum | solution.py:19
  36.2 8.2 %multiply_reduce_fusion.1 = f32[8,3,768]{2,1,0:T(4,128)S(1)} fusion(f32[8,4,256,768]{3,2,1,0:T(8,128)} %bitcast.187), kind=kLoop, calls=%fused_computation.1 | loop fusion | flops 9418752 | bytes 18948096 | tf_op jit(solution)/shard_map/reduce_sum | solution.py:19
  66.9 26.3 %collective-permute-done.13 = f32[7,768]{1,0:T(8,128)S(1)} collective-permute-done((f32[7,768]{1,0:T(8,128)S(1)}, f32[7,768]{1,0:T(8,128)S(1)}, u32[]{:S(2)}, u32[]{:S(2)}) %collective-permute-start.13) | collective-permute-done | bytes 21536 | tf_op jit(solution)/shard_map/ppermute | solution.py:15
  111.2 5.4 collective-permute-start.8
  143.7 4.3 collective-permute-done.23.piece_ref
  151.6 134.3 %collective-permute-done.22.piece_ref = bf16[1,256,768]{2,1,0:T(8,128)(2,1)S(1)} collective-permute-done((bf16[1,256,768]{2,1,0:T(8,128)(2,1)S(1)}, bf16[1,256,768]{2,1,0:T(8,128)(2,1)S(1)}, u32[]{:S(2)}, u32[]{:S(2)}) %collective-permute-start.22) | collective-permute-done | bytes 393248 | tf_op jit(solution)/shard_map/ppermute | solution.py:15
  290.7 72.3 %collective-permute-done.21.piece_ref = bf16[1,256,768]{2,1,0:T(8,128)(2,1)} collective-permute-done((bf16[1,256,768]{2,1,0:T(8,128)(2,1)S(1)}, bf16[1,256,768]{2,1,0:T(8,128)(2,1)}, u32[]{:S(2)}, u32[]{:S(2)}) %collective-permute-start.21) | collective-permute-done | bytes 393248 | tf_op jit(solution)/shard_map/ppermute | solution.py:15
  364.1 3.7 fusion.4
  381.4 81.1 %collective-permute-done.16.piece_ref = bf16[3,256,768]{2,1,0:T(8,128)(2,1)S(1)} collective-permute-done((bf16[3,256,768]{2,1,0:T(8,128)(2,1)S(1)}, bf16[3,256,768]{2,1,0:T(8,128)(2,1)S(1)}, u32[]{:S(2)}, u32[]{:S(2)}) %collective-permute-start.16) | collective-permute-done | bytes 1179680 | tf_op jit(solution)/shard_map/ppermute | solution.py:15
  462.5 4.9 collective-permute-start.31
  467.4 9.9 %collective-permute-done.14.piece_ref = bf16[3,256,768]{2,1,0:T(8,128)(2,1)S(1)} collective-permute-done((bf16[3,256,768]{2,1,0:T(8,128)(2,1)S(1)}, bf16[3,256,768]{2,1,0:T(8,128)(2,1)S(1)}, u32[]{:S(2)}, u32[]{:S(2)}) %collective-permute-start.14) | collective-permute-done | bytes 1179680 | tf_op jit(solution)/shard_map/ppermute | solution.py:15
  477.4 5.3 collective-permute-start.29
  482.7 5.7 collective-permute-start.28
  489.7 3.9 own.3.result_ref
  493.6 3.9 own.2.result_ref
  510.8 7.2 all_gather.3
  547.8 3.6 place.37.result_ref
  551.4 76.8 %collective-permute-done.31.piece_ref = bf16[4,256,768]{2,1,0:T(8,128)(2,1)} collective-permute-done((bf16[4,256,768]{2,1,0:T(8,128)(2,1)}, bf16[4,256,768]{2,1,0:T(8,128)(2,1)}, u32[]{:S(2)}, u32[]{:S(2)}) %collective-permute-start.31) | collective-permute-done | bytes 1572896 | tf_op jit(solution)/shard_map/ppermute | solution.py:15
  631.7 30.1 %collective-permute-done.30.piece_ref = bf16[4,256,768]{2,1,0:T(8,128)(2,1)} collective-permute-done((bf16[4,256,768]{2,1,0:T(8,128)(2,1)}, bf16[4,256,768]{2,1,0:T(8,128)(2,1)}, u32[]{:S(2)}, u32[]{:S(2)}) %collective-permute-start.30) | collective-permute-done | bytes 1572896 | tf_op jit(solution)/shard_map/ppermute | solution.py:15
  665.4 30.1 %collective-permute-done.29.piece_ref = bf16[4,256,768]{2,1,0:T(8,128)(2,1)} collective-permute-done((bf16[4,256,768]{2,1,0:T(8,128)(2,1)}, bf16[4,256,768]{2,1,0:T(8,128)(2,1)}, u32[]{:S(2)}, u32[]{:S(2)}) %collective-permute-start.29) | collective-permute-done | bytes 1572896 | tf_op jit(solution)/shard_map/ppermute | solution.py:15
  699.1 18.9 %collective-permute-done.28.piece_ref = bf16[4,256,768]{2,1,0:T(8,128)(2,1)} collective-permute-done((bf16[4,256,768]{2,1,0:T(8,128)(2,1)}, bf16[4,256,768]{2,1,0:T(8,128)(2,1)}, u32[]{:S(2)}, u32[]{:S(2)}) %collective-permute-start.28) | collective-permute-done | bytes 1572896 | tf_op jit(solution)/shard_map/ppermute | solution.py:15
  718.1 3.6 place.41
  (180 shorter events, 159.6 us)
Async XLA Ops:
  46.1 13.4 %collective-permute-start.1 = (f32[7,768]{1,0:T(8,128)S(1)}, f32[7,768]{1,0:T(8,128)S(1)}, u32[]{:S(2)}, u32[]{:S(2)}) collective-permute-start(f32[7,768]{1,0:T(8,128)S(1)} %get-tuple-element.68), channel_id=1, source_target_pairs={{0,5},{1,4},{2,7},{3,6},{4,1},{5,0},{6,3},{7,2},{8,13},{9,12},{10,... | collective-permute-start | bytes 64520 | tf_op jit(solution)/shard_map/ppermute | solution.py:15
  60.2 70.6 %collective-permute-start.27 = (bf16[1,256,768]{2,1,0:T(8,128)(2,1)S(1)}, bf16[1,256,768]{2,1,0:T(8,128)(2,1)S(1)}, u32[]{:S(2)}, u32[]{:S(2)}) collective-permute-start(bf16[1,256,768]{2,1,0:T(8,128)(2,1)S(1)} %fusion.33), channel_id=1, source_target_pairs={{0,4},{1,5},{2,6},{3,7},{4,0},{5,1},{6,2},{7,3},{8,12},{9,13},{10,... | collective-permute-start | bytes 1179656 | tf_op jit(solution)/shard_map/ppermute | solution.py:15
  62.1 74.9 %collective-permute-start.26 = (bf16[1,256,768]{2,1,0:T(8,128)(2,1)}, bf16[1,256,768]{2,1,0:T(8,128)(2,1)S(1)}, u32[]{:S(2)}, u32[]{:S(2)}) collective-permute-start(bf16[1,256,768]{2,1,0:T(8,128)(2,1)} %fusion.31), channel_id=1, source_target_pairs={{0,5},{1,4},{2,7},{3,6},{4,1},{5,0},{6,3},{7,2},{8,13},{9,12},{10,... | collective-permute-start | bytes 1179656 | tf_op jit(solution)/shard_map/ppermute | solution.py:15
  63.5 74.3 %collective-permute-start.25 = (bf16[1,256,768]{2,1,0:T(8,128)(2,1)S(1)}, bf16[1,256,768]{2,1,0:T(8,128)(2,1)S(1)}, u32[]{:S(2)}, u32[]{:S(2)}) collective-permute-start(bf16[1,256,768]{2,1,0:T(8,128)(2,1)S(1)} %fusion.35), channel_id=1, source_target_pairs={{0,1},{1,0},{2,3},{3,2},{4,5},{5,4},{6,7},{7,6},{8,9},{9,8},{10,11... | collective-permute-start | bytes 1179656 | tf_op jit(solution)/shard_map/ppermute | solution.py:15
  64.8 28.5 %collective-permute-start.13 = (f32[7,768]{1,0:T(8,128)S(1)}, f32[7,768]{1,0:T(8,128)S(1)}, u32[]{:S(2)}, u32[]{:S(2)}) collective-permute-start(f32[7,768]{1,0:T(8,128)S(1)} %fusion.59), channel_id=1, source_target_pairs={{0,4},{1,5},{2,6},{3,7},{4,0},{5,1},{6,2},{7,3},{8,12},{9,13},{10,... | collective-permute-start | bytes 64520 | tf_op jit(solution)/shard_map/ppermute | solution.py:15
  66.6 58.8 %collective-permute-start.36 = (bf16[2,256,32]{1,2,0:T(8,128)(2,1)S(1)}, bf16[2,256,32]{1,2,0:T(8,128)(2,1)S(1)}, u32[]{:S(2)}, u32[]{:S(2)}) collective-permute-start(bf16[2,256,32]{1,2,0:T(8,128)(2,1)S(1)} %pad_maximum_fusion.2), channel_id=1, source_target_pairs={{0,2},{1,3},{2,0},{3,1},{4,6},{5,7},{6,4},{7,5},{8,10},{9,11},{10,... | collective-permute-start | bytes 98312 | tf_op jit(solution)/shard_map/ppermute | solution.py:15
  123.5 18.9 %collective-permute-start.24 = (bf16[1,256,768]{2,1,0:T(8,128)(2,1)S(1)}, bf16[1,256,768]{2,1,0:T(8,128)(2,1)S(1)}, u32[]{:S(2)}, u32[]{:S(2)}) collective-permute-start(bf16[1,256,768]{2,1,0:T(8,128)(2,1)S(1)} %fusion.29), channel_id=1, source_target_pairs={{0,2},{1,3},{2,0},{3,1},{4,6},{5,7},{6,4},{7,5},{8,10},{9,11},{10,... | collective-permute-start | bytes 1179656 | tf_op jit(solution)/shard_map/ppermute | solution.py:15
  130.5 17.5 %collective-permute-start.23 = (bf16[1,256,768]{2,1,0:T(8,128)(2,1)}, bf16[1,256,768]{2,1,0:T(8,128)(2,1)S(1)}, u32[]{:S(2)}, u32[]{:S(2)}) collective-permute-start(bf16[1,256,768]{2,1,0:T(8,128)(2,1)} %fusion.27), channel_id=1, source_target_pairs={{0,3},{1,2},{2,1},{3,0},{4,7},{5,6},{6,5},{7,4},{8,11},{9,10},{10,... | collective-permute-start | bytes 1179656 | tf_op jit(solution)/shard_map/ppermute | solution.py:15
  131.5 232.6 %collective-permute-start.20 = (bf16[3,256,768]{2,1,0:T(8,128)(2,1)S(1)}, bf16[3,256,768]{2,1,0:T(8,128)(2,1)S(1)}, u32[]{:S(2)}, u32[]{:S(2)}) collective-permute-start(bf16[3,256,768]{2,1,0:T(8,128)(2,1)S(1)} %fusion.9), channel_id=1, source_target_pairs={{0,4},{1,5},{2,6},{3,7},{4,0},{5,1},{6,2},{7,3},{8,12},{9,13},{10,... | collective-permute-start | bytes 3538952 | tf_op jit(solution)/shard_map/ppermute | solution.py:15
  137.0 148.9 %collective-permute-start.22 = (bf16[1,256,768]{2,1,0:T(8,128)(2,1)S(1)}, bf16[1,256,768]{2,1,0:T(8,128)(2,1)S(1)}, u32[]{:S(2)}, u32[]{:S(2)}) collective-permute-start(bf16[1,256,768]{2,1,0:T(8,128)(2,1)S(1)} %fusion.25), channel_id=1, source_target_pairs={{0,6},{1,7},{2,4},{3,5},{4,2},{5,3},{6,0},{7,1},{8,14},{9,15},{10,... | collective-permute-start | bytes 1179656 | tf_op jit(solution)/shard_map/ppermute | solution.py:15
  137.8 230.0 %collective-permute-start.19 = (bf16[3,256,768]{2,1,0:T(8,128)(2,1)S(1)}, bf16[3,256,768]{2,1,0:T(8,128)(2,1)S(1)}, u32[]{:S(2)}, u32[]{:S(2)}) collective-permute-start(bf16[3,256,768]{2,1,0:T(8,128)(2,1)S(1)} %fusion.11), channel_id=1, source_target_pairs={{0,5},{1,4},{2,7},{3,6},{4,1},{5,0},{6,3},{7,2},{8,13},{9,12},{10,... | collective-permute-start | bytes 3538952 | tf_op jit(solution)/shard_map/ppermute | solution.py:15
  142.5 226.4 %collective-permute-start.18 = (bf16[3,256,768]{2,1,0:T(8,128)(2,1)S(1)}, bf16[3,256,768]{2,1,0:T(8,128)(2,1)S(1)}, u32[]{:S(2)}, u32[]{:S(2)}) collective-permute-start(bf16[3,256,768]{2,1,0:T(8,128)(2,1)S(1)} %fusion.13), channel_id=1, source_target_pairs={{0,6},{1,7},{2,4},{3,5},{4,2},{5,3},{6,0},{7,1},{8,14},{9,15},{10,... | collective-permute-start | bytes 3538952 | tf_op jit(solution)/shard_map/ppermute | solution.py:15
  148.7 221.7 %collective-permute-start.17 = (bf16[3,256,768]{2,1,0:T(8,128)(2,1)S(1)}, bf16[3,256,768]{2,1,0:T(8,128)(2,1)S(1)}, u32[]{:S(2)}, u32[]{:S(2)}) collective-permute-start(bf16[3,256,768]{2,1,0:T(8,128)(2,1)S(1)} %fusion.15), channel_id=1, source_target_pairs={{0,7},{1,6},{2,5},{3,4},{4,3},{5,2},{6,1},{7,0},{8,15},{9,14},{10,... | collective-permute-start | bytes 3538952 | tf_op jit(solution)/shard_map/ppermute | solution.py:15
  285.9 77.1 %collective-permute-start.21 = (bf16[1,256,768]{2,1,0:T(8,128)(2,1)S(1)}, bf16[1,256,768]{2,1,0:T(8,128)(2,1)}, u32[]{:S(2)}, u32[]{:S(2)}) collective-permute-start(bf16[1,256,768]{2,1,0:T(8,128)(2,1)S(1)} %fusion.23), channel_id=1, source_target_pairs={{0,7},{1,6},{2,5},{3,4},{4,3},{5,2},{6,1},{7,0},{8,15},{9,14},{10,... | collective-permute-start | bytes 1179656 | tf_op jit(solution)/shard_map/ppermute | solution.py:15
  362.9 114.4 %collective-permute-start.34 = (bf16[4,256,768]{2,1,0:T(8,128)(2,1)S(1)}, bf16[4,256,768]{2,1,0:T(8,128)(2,1)S(1)}, u32[]{:S(2)}, u32[]{:S(2)}) collective-permute-start(bf16[4,256,768]{2,1,0:T(8,128)(2,1)S(1)} %fusion.1), channel_id=1, source_target_pairs={{0,1},{1,0},{2,3},{3,2},{4,5},{5,4},{6,7},{7,6},{8,9},{9,8},{10,11... | collective-permute-start | bytes 4718600 | tf_op jit(solution)/shard_map/ppermute | solution.py:15
  364.1 118.6 %collective-permute-start.33 = (bf16[4,256,768]{2,1,0:T(8,128)(2,1)S(1)}, bf16[4,256,768]{2,1,0:T(8,128)(2,1)}, u32[]{:S(2)}, u32[]{:S(2)}) collective-permute-start(bf16[4,256,768]{2,1,0:T(8,128)(2,1)S(1)} %fusion.2), channel_id=1, source_target_pairs={{0,2},{1,3},{2,0},{3,1},{4,6},{5,7},{6,4},{7,5},{8,10},{9,11},{10,... | collective-permute-start | bytes 4718600 | tf_op jit(solution)/shard_map/ppermute | solution.py:15
  367.9 94.6 %collective-permute-start.16 = (bf16[3,256,768]{2,1,0:T(8,128)(2,1)S(1)}, bf16[3,256,768]{2,1,0:T(8,128)(2,1)S(1)}, u32[]{:S(2)}, u32[]{:S(2)}) collective-permute-start(bf16[3,256,768]{2,1,0:T(8,128)(2,1)S(1)} %fusion.17), channel_id=1, source_target_pairs={{0,1},{1,0},{2,3},{3,2},{4,5},{5,4},{6,7},{7,6},{8,9},{9,8},{10,11... | collective-permute-start | bytes 3538952 | tf_op jit(solution)/shard_map/ppermute | solution.py:15
  368.8 93.7 %collective-permute-start.15 = (bf16[3,256,768]{2,1,0:T(8,128)(2,1)S(1)}, bf16[3,256,768]{2,1,0:T(8,128)(2,1)S(1)}, u32[]{:S(2)}, u32[]{:S(2)}) collective-permute-start(bf16[3,256,768]{2,1,0:T(8,128)(2,1)S(1)} %fusion.19), channel_id=1, source_target_pairs={{0,2},{1,3},{2,0},{3,1},{4,6},{5,7},{6,4},{7,5},{8,10},{9,11},{10,... | collective-permute-start | bytes 3538952 | tf_op jit(solution)/shard_map/ppermute | solution.py:15
  370.4 106.9 %collective-permute-start.14 = (bf16[3,256,768]{2,1,0:T(8,128)(2,1)S(1)}, bf16[3,256,768]{2,1,0:T(8,128)(2,1)S(1)}, u32[]{:S(2)}, u32[]{:S(2)}) collective-permute-start(bf16[3,256,768]{2,1,0:T(8,128)(2,1)S(1)} %fusion.21), channel_id=1, source_target_pairs={{0,3},{1,2},{2,1},{3,0},{4,7},{5,6},{6,5},{7,4},{8,11},{9,10},{10,... | collective-permute-start | bytes 3538952 | tf_op jit(solution)/shard_map/ppermute | solution.py:15
  462.5 85.3 %collective-permute-start.32 = (bf16[4,256,768]{2,1,0:T(8,128)(2,1)}, bf16[4,256,768]{2,1,0:T(8,128)(2,1)}, u32[]{:S(2)}, u32[]{:S(2)}) collective-permute-start(bf16[4,256,768]{2,1,0:T(8,128)(2,1)} %fusion.3), channel_id=1, source_target_pairs={{0,3},{1,2},{2,1},{3,0},{4,7},{5,6},{6,5},{7,4},{8,11},{9,10},{10,... | collective-permute-start | bytes 4718600 | tf_op jit(solution)/shard_map/ppermute | solution.py:15
  462.5 165.6 %collective-permute-start.31 = (bf16[4,256,768]{2,1,0:T(8,128)(2,1)}, bf16[4,256,768]{2,1,0:T(8,128)(2,1)}, u32[]{:S(2)}, u32[]{:S(2)}) collective-permute-start(bf16[4,256,768]{2,1,0:T(8,128)(2,1)} %fusion.4), channel_id=1, source_target_pairs={{0,4},{1,5},{2,6},{3,7},{4,0},{5,1},{6,2},{7,3},{8,12},{9,13},{10,... | collective-permute-start | bytes 4718600 | tf_op jit(solution)/shard_map/ppermute | solution.py:15
  477.4 184.5 %collective-permute-start.30 = (bf16[4,256,768]{2,1,0:T(8,128)(2,1)}, bf16[4,256,768]{2,1,0:T(8,128)(2,1)}, u32[]{:S(2)}, u32[]{:S(2)}) collective-permute-start(bf16[4,256,768]{2,1,0:T(8,128)(2,1)} %fusion.5), channel_id=1, source_target_pairs={{0,5},{1,4},{2,7},{3,6},{4,1},{5,0},{6,3},{7,2},{8,13},{9,12},{10,... | collective-permute-start | bytes 4718600 | tf_op jit(solution)/shard_map/ppermute | solution.py:15
  477.4 218.2 %collective-permute-start.29 = (bf16[4,256,768]{2,1,0:T(8,128)(2,1)}, bf16[4,256,768]{2,1,0:T(8,128)(2,1)}, u32[]{:S(2)}, u32[]{:S(2)}) collective-permute-start(bf16[4,256,768]{2,1,0:T(8,128)(2,1)} %fusion.6), channel_id=1, source_target_pairs={{0,6},{1,7},{2,4},{3,5},{4,2},{5,3},{6,0},{7,1},{8,14},{9,15},{10,... | collective-permute-start | bytes 4718600 | tf_op jit(solution)/shard_map/ppermute | solution.py:15
  482.7 235.3 %collective-permute-start.28 = (bf16[4,256,768]{2,1,0:T(8,128)(2,1)}, bf16[4,256,768]{2,1,0:T(8,128)(2,1)}, u32[]{:S(2)}, u32[]{:S(2)}) collective-permute-start(bf16[4,256,768]{2,1,0:T(8,128)(2,1)} %fusion.7), channel_id=1, source_target_pairs={{0,7},{1,6},{2,5},{3,4},{4,3},{5,2},{6,1},{7,0},{8,15},{9,14},{10,... | collective-permute-start | bytes 4718600 | tf_op jit(solution)/shard_map/ppermute | solution.py:15
  (32 other events, 350.3 us)
